TPU v7x, 32 devices: a whole 2x2x4 slice. The times are simulated.
32 devices in a mesh: movie: 16 (over z, y, x), user: 2 (over core).
Axes of the slice: x: 2, y: 2, z: 4, core: 2. Of those that a mesh axis runs over, the one named last changes fastest.
Arguments:
- movie_ids: int32 [128, 128], P(('movie', 'user')), may hold values from 0 to 17919, as said below
- ratings: int32 [128, 128], P(('movie', 'user')), may hold values from 0 to 4
- valid: int32 [128, 128], P(('movie', 'user')), may hold values from 0 to 1, as said below
- weights: bfloat16 [5, 17920, 1024], P(None, 'movie'), may hold values from -0.5 to 0.5
- vis_bias: float32 [5, 17920], P(None, 'movie'), may hold values from -5 to 260
- hid_bias: float32 [1024], replicated, may hold values from -5 to 5
Outputs:
- weight_grad: float32 [5, 17920, 1024], P(None, 'movie')
- visible_grad: float32 [5, 17920], P(None, 'movie')
- hidden_grad: float32 [1024], replicated
- positive_hidden: float32 [128, 1024], P(('movie', 'user'))
Inputs may be any that keep to these rules, and one draw needn't show every extreme that they name: `movie_ids`: movie ids within one user's block are distinct. Of the slots with valid 1 among the users of one device (4 consecutive users), at most 96 name movies of any one block of 1120 consecutive movie ids; in every draw some such block takes exactly 96 from the users of every device. Slots with valid 0 are padding and count nowhere.
All inputs are finite; a program needn't handle non-finite values.
Results may differ from a plain program's by a relative error of at most 0.0054.
Values may be sent and summed in bfloat16 or wider, within the bound.
No kernel may reach another device: no remote copies, remote signals or barrier semaphores. Data moves between devices by JAX's collectives and lax.ppermute only.
A program may use at most 128 MiB of HBM per device.

v0:
```python
import jax
import jax.numpy as jnp
from jax import lax
from jax.sharding import PartitionSpec as P


def reconstruct(hidden_rows, weight_table, bias_row, rated_mask, levels):
    group_rows = hidden_rows.shape[0]
    rating_logits = (
        lax.dot_general(
            hidden_rows, weight_table, (((1,), (1,)), ((), ())), preferred_element_type=jnp.float32
        )
        + bias_row[None, :]
    )
    shaped = rating_logits.reshape(group_rows, levels, -1)
    largest = jnp.max(shaped, axis=1, keepdims=True)
    exponent = jnp.exp(shaped - largest)
    softened = (exponent / jnp.sum(exponent, axis=1, keepdims=True)).astype(jnp.bfloat16)
    return (softened * rated_mask[:, None, :]).reshape(group_rows, -1)


def hidden_phase(visible, weight_table, hid_bias, local_users, device_index):
    combined = jnp.dot(visible, weight_table, preferred_element_type=jnp.float32)
    all_probs = jax.nn.sigmoid(hid_bias[None, :] + lax.psum(combined, "movie"))
    own_rows = lax.dynamic_slice_in_dim(all_probs, device_index * local_users, local_users, 0)
    return (own_rows, all_probs.astype(jnp.bfloat16))


def on_device(movie_ids, ratings, valid, weights, vis_bias, hid_bias):
    owners = lax.axis_size("movie")
    device_index = lax.axis_index("movie")
    local_users, slot_count = movie_ids.shape
    levels, local_movies, hidden = weights.shape
    columns = levels * local_movies
    group_rows = owners * local_users
    capacity = max(2, 3 * local_users * slot_count // owners)
    flat_ids = movie_ids.reshape(-1)
    owner_ids = flat_ids // local_movies
    column_ids = ratings.reshape(-1) * local_movies + flat_ids % local_movies
    user_ids = jnp.arange(local_users * slot_count, dtype=jnp.int32) // slot_count
    usable = valid.reshape(-1) == 1
    matches = (owner_ids[:, None] == jnp.arange(owners, dtype=jnp.int32)[None, :]) & usable[:, None]
    ranking = jnp.cumsum(matches.astype(jnp.int32), axis=0) - 1
    placed = jnp.sum(jnp.where(matches, ranking, 0), axis=1)
    target = jnp.where(usable, owner_ids, owners)
    user_slots = (
        jnp.zeros((owners, capacity), jnp.int32).at[target, placed].set(user_ids, mode="drop")
    )
    column_slots = (
        jnp.full((owners, capacity), -1, jnp.int32).at[target, placed].set(column_ids, mode="drop")
    )
    got_users, got_columns = (
        lax.all_to_all(user_slots, "movie", split_axis=0, concat_axis=0, tiled=True),
        lax.all_to_all(column_slots, "movie", split_axis=0, concat_axis=0, tiled=True),
    )
    user_hot = (got_users[:, :, None] == jnp.arange(local_users, dtype=jnp.int32)).astype(
        jnp.bfloat16
    )
    column_hot = (got_columns[:, :, None] == jnp.arange(columns, dtype=jnp.int32)).astype(
        jnp.bfloat16
    )
    shown = jnp.einsum("ncu,ncj->nuj", user_hot, column_hot, preferred_element_type=jnp.float32)
    shown = shown.reshape(group_rows, columns).astype(jnp.bfloat16)
    rated_mask = jnp.sum(shown.reshape(group_rows, levels, local_movies), axis=1)
    weight_table = weights.reshape(columns, hidden)
    positive_own, positive_group = hidden_phase(
        shown, weight_table, hid_bias, local_users, device_index
    )
    reconstructed_ratings = reconstruct(
        positive_group, weight_table, vis_bias.reshape(columns), rated_mask, levels
    )
    negative_own, negative_group = hidden_phase(
        reconstructed_ratings, weight_table, hid_bias, local_users, device_index
    )
    contract = (((0,), (0,)), ((), ()))
    weight_grad = lax.dot_general(
        shown, positive_group, contract, preferred_element_type=jnp.float32
    )
    weight_grad = weight_grad - lax.dot_general(
        reconstructed_ratings, negative_group, contract, preferred_element_type=jnp.float32
    )
    visible_grad = jnp.sum(shown.astype(jnp.float32), axis=0) - jnp.sum(
        reconstructed_ratings.astype(jnp.float32), axis=0
    )
    weight_grad, visible_grad = lax.psum((weight_grad, visible_grad), "user")
    hidden_grad = lax.psum(jnp.sum(positive_own - negative_own, axis=0), ("movie", "user"))
    return (
        weight_grad.reshape(levels, local_movies, hidden),
        visible_grad.reshape(levels, local_movies),
        hidden_grad,
        positive_own,
    )


def solution(mesh):
    in_specs = (
        P(("movie", "user"), None),
        P(("movie", "user"), None),
        P(("movie", "user"), None),
        P(None, "movie", None),
        P(None, "movie"),
        P(),
    )
    out_specs = (P(None, "movie", None), P(None, "movie"), P(), P(("movie", "user"), None))
    return jax.shard_map(
        on_device, mesh=mesh, in_specs=in_specs, out_specs=out_specs, check_vma=False
    )
```

profile of v0, /device:TPU:0, one launch (start us, length us, event | category | flops | bytes accessed | tf_op | source)
XLA Modules:
  0.0 498.8 jit_solution(16229236096760497218)
XLA Ops:
  9.9 0.7 fusion.18
  10.7 1.2 reduce-window.6
  12.8 70.4 %scatter_fusion.1 = s32[16,96]{1,0:T(8,128)} fusion(s32[16,96]{1,0:T(8,128)} %broadcast_in_dim.15, s32[512]{0:T(512)S(1)} %bitcast.81, s32[512]{0:T(512)S(1)} %get-tuple-element.10), kind=kCustom, calls=%fused_computation.1 | custom fusion | bytes 10240 | tf_op jit(solution)/shard_map/scatter | solution.py:50
  83.2 8.4 %all-to-all-start.1 = ((s32[16,1,96]{2,1,0:T(1,128)}), s32[16,1,96]{2,1,0:T(1,128)S(1)}, u32[]{:S(2)}, u32[]{:S(2)}) async-start(s32[16,1,96]{2,1,0:T(1,128)} %bitcast.13), calls=%async_computation.1 | async-start | bytes 16384 | tf_op jit(solution)/shard_map/all_to_all | solution.py:54
  91.7 25.2 %scatter_fusion = s32[16,96]{1,0:T(8,128)S(1)} fusion(s32[16,96]{1,0:T(8,128)S(1)} %broadcast_in_dim.12, s32[512]{0:T(512)S(1)} %bitcast.82, s32[512]{0:T(512)S(1)} %add_select_fusion.1), kind=kCustom, calls=%fused_computation | custom fusion | bytes 10240 | tf_op jit(solution)/shard_map/scatter | solution.py:47
  116.9 14.0 %all_to_all.18 = s32[16,1,96]{2,1,0:T(1,128)S(1)} all-to-all(s32[16,1,96]{2,1,0:T(1,128)S(1)} %bitcast.75), channel_id=1, replica_groups=mesh['movie'=16,'user'=2] {'movie'}, dimensions={0} | all-to-all | bytes 12288 | tf_op jit(solution)/shard_map/all_to_all | solution.py:53
  130.9 6.6 %convert_reduce_fusion.1 = (f32[5600]{0:T(1024)S(1)}, bf16[16,4,5600]{2,1,0:T(4,128)(2,1)S(1)}) fusion(s32[16,96]{1,0:T(8,128)S(1)} %bitcast.85, s32[16,96]{1,0:T(8,128)S(1)} %bitcast.86), kind=kOutput, calls=%fused_computation.12 | convolution fusion | flops 78490144 | bytes 751488 | tf_op jit(solution)/shard_map/ncu,ncj->nuj/dot_general | solution.py:62
  137.8 7.3 %fusion.24 = f32[64,1024]{1,0:T(8,128)} fusion(bf16[64,5600]{1,0:T(8,128)(2,1)S(1)} %convert_element_type.42, bf16[5600,1024]{1,0:T(8,128)(2,1)} %bitcast.77), kind=kOutput, calls=%fused_computation.65 | convolution fusion | flops 734003200 | bytes 12447744 | tf_op jit(solution)/shard_map/dot_general | solution.py:23
  145.5 0.9 convert_element_type.45
  146.4 0.8 reduce_sum.62
  147.2 1.1 mul.26
  148.3 2.7 mul.27
  151.1 98.4 %all-reduce.4.cloned.1.call-done = f32[64,1024]{1,0:T(8,128)} async-done(((f32[64,1024]{1,0:T(8,128)}), f32[64,1024]{1,0:T(8,128)}) %all-reduce.4.cloned.1.call-update) | async-done | bytes 262160 | tf_op jit(solution)/shard_map/psum | solution.py:24
  249.4 1.0 add_divide_fusion.1
  250.5 11.1 %fusion.9 = f32[5600,1024]{1,0:T(8,128)} fusion(bf16[64,5600]{1,0:T(8,128)(2,1)} %copy-done.1, f32[64,1024]{1,0:T(8,128)S(1)} %add_divide_fusion.1), kind=kOutput, calls=%fused_computation.22 | convolution fusion | flops 734068736 | bytes 23916544 | tf_op jit(solution)/shard_map/dot_general | solution.py:76
  261.7 4.7 convolution_add_fusion
  266.4 1.9 reshape.182
  268.3 0.7 reduce_max.9
  269.0 1.0 fusion.3
  270.0 0.8 fusion.4
  270.8 7.1 %convolution_bitcast_fusion = f32[64,1024]{1,0:T(8,128)} fusion(bf16[5,1120,1024]{2,1,0:T(8,128)(2,1)} %param.9, bf16[64,5,1120]{2,1,0:T(8,128)(2,1)S(1)} %fusion.4), kind=kOutput, calls=%fused_computation.15 | convolution fusion | flops 734003200 | bytes 12447744 | tf_op jit(solution)/shard_map/dot_general | solution.py:23
  278.3 1.6 sub.52
  280.0 1.6 div.54
  281.5 3.0 div.55
  284.5 3.0 convert_reduce_fusion
  287.5 97.3 %all-reduce.6.cloned.1.call-done = f32[64,1024]{1,0:T(8,128)} async-done(((f32[64,1024]{1,0:T(8,128)}), f32[64,1024]{1,0:T(8,128)}) %all-reduce.6.cloned.1.call-update) | async-done | bytes 262160 | tf_op jit(solution)/shard_map/psum | solution.py:24
  384.8 1.0 add_divide_fusion
  385.8 15.5 %convolution_subtract_fusion = f32[5600,1024]{1,0:T(8,128)} fusion(f32[5600,1024]{1,0:T(8,128)} %fusion.9, bf16[64,5600]{1,0:T(8,128)(2,1)} %get-tuple-element.7, f32[64,1024]{1,0:T(8,128)S(1)} %add_divide_fusion), kind=kOutput, calls=%fused_computation.5 | convolution fusion | flops 739803136 | bytes 46854144 | tf_op jit(solution)/shard_map/dot_general | solution.py:79
  401.4 4.0 psum.38
  406.1 39.4 %psum.39 = f32[1024]{0:T(1024)} all-reduce(f32[1024]{0:T(1024)S(1)} %get-tuple-element.4), channel_id=1, replica_groups=mesh['movie'=16,'user'=2] {'movie','user'}, use_global_device_ids=true, to_apply=%region_15.16 | all-reduce | flops 1024 | bytes 8192 | tf_op jit(solution)/shard_map/psum | solution.py:86
  445.4 30.3 %all-reduce.8.cloned.1.call-done = f32[5,1120,1024]{2,1,0:T(8,128)} async-done(((f32[5,1120,1024]{2,1,0:T(8,128)}), f32[5,1120,1024]{2,1,0:T(8,128)}) %all-reduce.8.cloned.1.call-update) | async-done | bytes 22937616 | tf_op jit(solution)/shard_map/psum | solution.py:85
  475.8 16.5 %copy.37 = f32[5,1120,1024]{2,1,0:T(8,128)} copy(f32[5,1120,1024]{2,1,0:T(8,128)} %all-reduce.8.cloned.1.call-done) | data formatting | bytes 45875200
  (43 shorter events, 5.6 us)
Async XLA Ops:
  83.2 33.7 %all-to-all-start.1 = ((s32[16,1,96]{2,1,0:T(1,128)}), s32[16,1,96]{2,1,0:T(1,128)S(1)}, u32[]{:S(2)}, u32[]{:S(2)}) async-start(s32[16,1,96]{2,1,0:T(1,128)} %bitcast.13), calls=%async_computation.1 | async-start | bytes 16384 | tf_op jit(solution)/shard_map/all_to_all | solution.py:54
  91.6 157.9 %all-reduce.4.cloned.1.call-start = ((), (), s32[]{:S(2)}) async-start(), calls=%async_computation.2 | async-start | bytes 524288 | tf_op jit(solution)/shard_map/psum | solution.py:24
  137.8 7.4 %copy-start.1 = (bf16[64,5600]{1,0:T(8,128)(2,1)}, bf16[64,5600]{1,0:T(8,128)(2,1)S(1)}, u32[]{:S(2)}) copy-start(bf16[64,5600]{1,0:T(8,128)(2,1)S(1)} %convert_element_type.42) | copy-start | bytes 2150404
  137.8 7.6 %copy-start.3 = (f32[5,1120]{1,0:T(8,128)S(1)}, f32[5,1120]{1,0:T(8,128)}, u32[]{:S(2)}) copy-start(f32[5,1120]{1,0:T(8,128)} %param.10) | copy-start | bytes 67204
  145.2 239.6 %all-reduce.6.cloned.1.call-start = ((), (), s32[]{:S(2)}) async-start(), calls=%async_computation.3 | async-start | bytes 524288 | tf_op jit(solution)/shard_map/psum | solution.py:24
  146.4 103.1 %copy-start.4 = (f32[1024]{0:T(1024)S(1)}, f32[1024]{0:T(1024)}, u32[]{:S(2)}) copy-start(f32[1024]{0:T(1024)} %param.11) | copy-start | bytes 12292
  148.3 113.3 %slice-start = ((s8[11468800]{0:T(1024)(128)(4,1)}), s8[3080192]{0:T(1024)(128)(4,1)S(1)}, s32[]{:S(2)}) async-start(s8[11468800]{0:T(1024)(128)(4,1)} %bitcast.78), calls=%async_computation.5 | async-start | bytes 6160384
  250.5 11.2 %slice-start.1 = ((s8[11468800]{0:T(1024)(128)(4,1)}), s8[4194304]{0:T(1024)(128)(4,1)S(1)}, s32[]{:S(2)}) async-start(s8[11468800]{0:T(1024)(128)(4,1)} %bitcast.78), calls=%async_computation.6 | async-start | bytes 8388608
  250.5 11.2 %slice-start.2 = ((s8[11468800]{0:T(1024)(128)(4,1)}), s8[4194304]{0:T(1024)(128)(4,1)S(1)}, s32[]{:S(2)}) async-start(s8[11468800]{0:T(1024)(128)(4,1)} %bitcast.78), calls=%async_computation.7 | async-start | bytes 8388608
  277.9 197.9 %all-reduce.8.cloned.1.call-start = ((), (), s32[]{:S(2)}) async-start(), calls=%async_computation.4 | async-start | bytes 45875200 | tf_op jit(solution)/shard_map/psum | solution.py:85
  281.5 3.0 copy-start
  281.5 3.0 copy-start.2
Sparse Core Ops, SparseCore 0:
  145.3 104.1 all-reduce.3
  278.0 106.6 all-reduce.5
  401.4 74.2 all-reduce.7
where the time goes:
time: 501 us; the launch traced here: 499 us
  waiting for transfers between devices  226 us (45%)
  local copies, waits for them, and re-layouts  126 us (25%)
  blocking collectives  57.4 us (11%)
  matrix products  52.3 us (10%)
  between operations  14 us (3%)
  other arithmetic  13.7 us (3%)
  starting transfers between devices  8.93 us (2%)
    psum x2, waiting for transfers between devices, hidden_phase(): all_probs = jax.nn.sigmoid(hid_bias[None, :] + lax.psum(combined, 'movie'))  196 us
    scatter x1, local copies, waits for them, and re-layouts, on_device(): jnp.full((owners, capacity), -1, jnp.int32).at[target, placed]  70.4 us
    psum x1, blocking collectives, on_device(): lax.psum(jnp.sum(positive_own - negative_own, axis=0), ('movie', 'user'))  39.4 us
    psum x1, waiting for transfers between devices, on_device(): weight_grad, visible_grad = lax.psum((weight_grad, visible_grad), 'user')  30.3 us
    scatter x1, local copies, waits for them, and re-layouts, on_device(): jnp.zeros((owners, capacity), jnp.int32).at[target, placed]  25.2 us
    unnamed x17, local copies, waits for them, and re-layouts  16.6 us
    dot_general x1, matrix products, on_device(): lax.dot_general(reconstructed_ratings, negative_group, contract, preferre...  15.5 us
    dot_general x2, matrix products, hidden_phase(): jnp.dot(visible, weight_table, preferred_element_type=jnp.float32)  14.4 us
  transfers between devices with their start and end apart: 4, of which 3 were waited for; matrix products, arithmetic and copies ran while one was open for 8% of the time, Pallas kernels for 0%

commit v1 on v0

--- a/solution.py
+++ b/solution.py
@@ -83,7 +83,7 @@
         reconstructed_ratings.astype(jnp.float32), axis=0
     )
     weight_grad, visible_grad = lax.psum((weight_grad, visible_grad), "user")
-    hidden_grad = lax.psum(jnp.sum(positive_own - negative_own, axis=0), ("movie", "user"))
+    hidden_grad = lax.psum(lax.psum(jnp.sum(positive_own - negative_own, axis=0), "user"), "movie")
     return (
         weight_grad.reshape(levels, local_movies, hidden),
         visible_grad.reshape(levels, local_movies),

time: 501 us -> 501 us (level)
  no operation moved by 1% of the time
where the time goes in v1:
time: 501 us; the launch traced here: 499 us
  waiting for transfers between devices  225 us (45%)
  local copies, waits for them, and re-layouts  126 us (25%)
  blocking collectives  58.4 us (12%)
  matrix products  52.3 us (10%)
  between operations  14 us (3%)
  other arithmetic  13.7 us (3%)
  starting transfers between devices  8.93 us (2%)
    psum x2, waiting for transfers between devices, hidden_phase(): all_probs = jax.nn.sigmoid(hid_bias[None, :] + lax.psum(combined, 'movie'))  196 us
    scatter x1, local copies, waits for them, and re-layouts, on_device(): jnp.full((owners, capacity), -1, jnp.int32).at[target, placed]  70.4 us
    psum x1, blocking collectives, on_device(): lax.psum(lax.psum(jnp.sum(positive_own - negative_own, axis=0), 'user'),...  40.4 us
    psum x1, waiting for transfers between devices, on_device(): weight_grad, visible_grad = lax.psum((weight_grad, visible_grad), 'user')  29.4 us
    scatter x1, local copies, waits for them, and re-layouts, on_device(): jnp.zeros((owners, capacity), jnp.int32).at[target, placed]  25.2 us
    unnamed x17, local copies, waits for them, and re-layouts  16.6 us
    dot_general x1, matrix products, on_device(): lax.dot_general(reconstructed_ratings, negative_group, contract, preferre...  15.5 us
    dot_general x2, matrix products, hidden_phase(): jnp.dot(visible, weight_table, preferred_element_type=jnp.float32)  14.4 us
  transfers between devices with their start and end apart: 4, of which 3 were waited for; matrix products, arithmetic and copies ran while one was open for 8% of the time, Pallas kernels for 0%

profile of v1, /device:TPU:0, one launch (start us, length us, event | category | flops | bytes accessed | tf_op | source)
XLA Modules:
  0.0 498.8 jit_solution(11637472938053155691)
XLA Ops:
  9.9 0.7 fusion.18
  10.7 1.2 reduce-window.6
  12.8 70.4 %scatter_fusion.1 = s32[16,96]{1,0:T(8,128)} fusion(s32[16,96]{1,0:T(8,128)} %broadcast_in_dim.15, s32[512]{0:T(512)S(1)} %bitcast.81, s32[512]{0:T(512)S(1)} %get-tuple-element.12), kind=kCustom, calls=%fused_computation.1 | custom fusion | bytes 10240 | tf_op jit(solution)/shard_map/scatter | solution.py:50
  83.2 8.4 %all-to-all-start.1 = ((s32[16,1,96]{2,1,0:T(1,128)}), s32[16,1,96]{2,1,0:T(1,128)S(1)}, u32[]{:S(2)}, u32[]{:S(2)}) async-start(s32[16,1,96]{2,1,0:T(1,128)} %bitcast.13), calls=%async_computation.1 | async-start | bytes 16384 | tf_op jit(solution)/shard_map/all_to_all | solution.py:54
  91.7 25.2 %scatter_fusion = s32[16,96]{1,0:T(8,128)S(1)} fusion(s32[16,96]{1,0:T(8,128)S(1)} %broadcast_in_dim.12, s32[512]{0:T(512)S(1)} %bitcast.82, s32[512]{0:T(512)S(1)} %add_select_fusion.1), kind=kCustom, calls=%fused_computation | custom fusion | bytes 10240 | tf_op jit(solution)/shard_map/scatter | solution.py:47
  116.9 14.0 %all_to_all.18 = s32[16,1,96]{2,1,0:T(1,128)S(1)} all-to-all(s32[16,1,96]{2,1,0:T(1,128)S(1)} %bitcast.75), channel_id=1, replica_groups=mesh['movie'=16,'user'=2] {'movie'}, dimensions={0} | all-to-all | bytes 12288 | tf_op jit(solution)/shard_map/all_to_all | solution.py:53
  130.9 6.6 %convert_reduce_fusion.1 = (f32[5600]{0:T(1024)S(1)}, bf16[16,4,5600]{2,1,0:T(4,128)(2,1)S(1)}) fusion(s32[16,96]{1,0:T(8,128)S(1)} %bitcast.85, s32[16,96]{1,0:T(8,128)S(1)} %bitcast.86), kind=kOutput, calls=%fused_computation.12 | convolution fusion | flops 78490144 | bytes 751488 | tf_op jit(solution)/shard_map/ncu,ncj->nuj/dot_general | solution.py:62
  137.8 7.3 %fusion.24 = f32[64,1024]{1,0:T(8,128)} fusion(bf16[64,5600]{1,0:T(8,128)(2,1)S(1)} %convert_element_type.42, bf16[5600,1024]{1,0:T(8,128)(2,1)} %bitcast.77), kind=kOutput, calls=%fused_computation.65 | convolution fusion | flops 734003200 | bytes 12447744 | tf_op jit(solution)/shard_map/dot_general | solution.py:23
  145.5 0.9 convert_element_type.45
  146.4 0.8 reduce_sum.62
  147.2 1.1 mul.26
  148.3 2.7 mul.27
  151.1 98.4 %all-reduce.5.cloned.1.call-done = f32[64,1024]{1,0:T(8,128)} async-done(((f32[64,1024]{1,0:T(8,128)}), f32[64,1024]{1,0:T(8,128)}) %all-reduce.5.cloned.1.call-update) | async-done | bytes 262160 | tf_op jit(solution)/shard_map/psum | solution.py:24
  249.4 1.0 add_divide_fusion.1
  250.5 11.1 %fusion.9 = f32[5600,1024]{1,0:T(8,128)} fusion(bf16[64,5600]{1,0:T(8,128)(2,1)} %copy-done.1, f32[64,1024]{1,0:T(8,128)S(1)} %add_divide_fusion.1), kind=kOutput, calls=%fused_computation.22 | convolution fusion | flops 734068736 | bytes 23916544 | tf_op jit(solution)/shard_map/dot_general | solution.py:76
  261.7 4.7 convolution_add_fusion
  266.4 1.9 reshape.182
  268.3 0.7 reduce_max.9
  269.0 1.0 fusion.3
  270.0 0.8 fusion.4
  270.8 7.1 %convolution_bitcast_fusion = f32[64,1024]{1,0:T(8,128)} fusion(bf16[5,1120,1024]{2,1,0:T(8,128)(2,1)} %param.9, bf16[64,5,1120]{2,1,0:T(8,128)(2,1)S(1)} %fusion.4), kind=kOutput, calls=%fused_computation.15 | convolution fusion | flops 734003200 | bytes 12447744 | tf_op jit(solution)/shard_map/dot_general | solution.py:23
  278.3 1.6 sub.52
  280.0 1.6 div.54
  281.5 3.0 div.55
  284.5 3.0 convert_reduce_fusion
  287.5 97.3 %all-reduce.7.cloned.1.call-done = f32[64,1024]{1,0:T(8,128)} async-done(((f32[64,1024]{1,0:T(8,128)}), f32[64,1024]{1,0:T(8,128)}) %all-reduce.7.cloned.1.call-update) | async-done | bytes 262160 | tf_op jit(solution)/shard_map/psum | solution.py:24
  384.8 1.0 add_divide_fusion
  385.8 15.5 %convolution_subtract_fusion = f32[5600,1024]{1,0:T(8,128)} fusion(f32[5600,1024]{1,0:T(8,128)} %fusion.9, bf16[64,5600]{1,0:T(8,128)(2,1)} %get-tuple-element.9, f32[64,1024]{1,0:T(8,128)S(1)} %add_divide_fusion), kind=kOutput, calls=%fused_computation.5 | convolution fusion | flops 739803136 | bytes 46854144 | tf_op jit(solution)/shard_map/dot_general | solution.py:79
  402.0 4.0 all-reduce
  406.1 40.4 %psum.47 = f32[1024]{0:T(1024)} all-reduce(f32[1024]{0:T(1024)S(1)} %get-tuple-element.5), channel_id=1, replica_groups=mesh['movie'=16,'user'=2] {'movie'}, use_global_device_ids=true, to_apply=%region_16.17 | all-reduce | flops 1024 | bytes 8192 | tf_op jit(solution)/shard_map/psum | solution.py:86
  446.4 29.4 %all-reduce.9.cloned.1.call-done = f32[5,1120,1024]{2,1,0:T(8,128)} async-done(((f32[5,1120,1024]{2,1,0:T(8,128)}), f32[5,1120,1024]{2,1,0:T(8,128)}) %all-reduce.9.cloned.1.call-update) | async-done | bytes 22937616 | tf_op jit(solution)/shard_map/psum | solution.py:85
  475.8 16.5 %copy.37 = f32[5,1120,1024]{2,1,0:T(8,128)} copy(f32[5,1120,1024]{2,1,0:T(8,128)} %all-reduce.9.cloned.1.call-done) | data formatting | bytes 45875200
  (43 shorter events, 5.6 us)
Async XLA Ops:
  83.2 33.7 %all-to-all-start.1 = ((s32[16,1,96]{2,1,0:T(1,128)}), s32[16,1,96]{2,1,0:T(1,128)S(1)}, u32[]{:S(2)}, u32[]{:S(2)}) async-start(s32[16,1,96]{2,1,0:T(1,128)} %bitcast.13), calls=%async_computation.1 | async-start | bytes 16384 | tf_op jit(solution)/shard_map/all_to_all | solution.py:54
  91.6 157.9 %all-reduce.5.cloned.1.call-start = ((), (), s32[]{:S(2)}) async-start(), calls=%async_computation.2 | async-start | bytes 524288 | tf_op jit(solution)/shard_map/psum | solution.py:24
  137.8 7.4 %copy-start.1 = (bf16[64,5600]{1,0:T(8,128)(2,1)}, bf16[64,5600]{1,0:T(8,128)(2,1)S(1)}, u32[]{:S(2)}) copy-start(bf16[64,5600]{1,0:T(8,128)(2,1)S(1)} %convert_element_type.42) | copy-start | bytes 2150404
  137.8 7.6 %copy-start.3 = (f32[5,1120]{1,0:T(8,128)S(1)}, f32[5,1120]{1,0:T(8,128)}, u32[]{:S(2)}) copy-start(f32[5,1120]{1,0:T(8,128)} %param.10) | copy-start | bytes 67204
  145.2 239.6 %all-reduce.7.cloned.1.call-start = ((), (), s32[]{:S(2)}) async-start(), calls=%async_computation.3 | async-start | bytes 524288 | tf_op jit(solution)/shard_map/psum | solution.py:24
  146.4 103.1 %copy-start.4 = (f32[1024]{0:T(1024)S(1)}, f32[1024]{0:T(1024)}, u32[]{:S(2)}) copy-start(f32[1024]{0:T(1024)} %param.11) | copy-start | bytes 12292
  148.3 113.3 %slice-start = ((s8[11468800]{0:T(1024)(128)(4,1)}), s8[3080192]{0:T(1024)(128)(4,1)S(1)}, s32[]{:S(2)}) async-start(s8[11468800]{0:T(1024)(128)(4,1)} %bitcast.78), calls=%async_computation.5 | async-start | bytes 6160384
  250.5 11.2 %slice-start.1 = ((s8[11468800]{0:T(1024)(128)(4,1)}), s8[4194304]{0:T(1024)(128)(4,1)S(1)}, s32[]{:S(2)}) async-start(s8[11468800]{0:T(1024)(128)(4,1)} %bitcast.78), calls=%async_computation.6 | async-start | bytes 8388608
  250.5 11.2 %slice-start.2 = ((s8[11468800]{0:T(1024)(128)(4,1)}), s8[4194304]{0:T(1024)(128)(4,1)S(1)}, s32[]{:S(2)}) async-start(s8[11468800]{0:T(1024)(128)(4,1)} %bitcast.78), calls=%async_computation.7 | async-start | bytes 8388608
  277.9 197.9 %all-reduce.9.cloned.1.call-start = ((), (), s32[]{:S(2)}) async-start(), calls=%async_computation.4 | async-start | bytes 45875200 | tf_op jit(solution)/shard_map/psum | solution.py:85
  281.5 3.0 copy-start
  281.5 3.0 copy-start.2
Sparse Core Ops, SparseCore 0:
  145.3 104.1 all-reduce.4
  278.0 106.6 all-reduce.6
  401.4 74.3 all-reduce.8
